TPU v7x, 32 devices: a whole 2x2x4 slice. The times are simulated.
32 devices in a mesh: dp: 2 (over y), row: 4 (over x, core), col: 4 (over z).
Axes of the slice: x: 2, y: 2, z: 4, core: 2. Of those that a mesh axis runs over, the one named last changes fastest.
Arguments:
- tokens: bfloat16 [2048, 8192], P(('dp', 'col'), 'row'), may hold values from -6 to 6
- frozen_weight: bfloat16 [8192, 8192], P('row', 'col'), may hold values from -0.0625 to 0.0625
- input_adapter_factor: bfloat16 [16, 8192], P(None, 'row'), may hold values from -0.0625 to 0.0625
- output_adapter_factor: bfloat16 [16, 8192], P(None, 'col'), may hold values from -1.5 to 1.5
- magnitude: float32 [8192], P('col'), may hold values from 0.5 to 2
- cotangent: bfloat16 [2048, 8192], P(('dp', 'row'), 'col'), may hold values from -6 to 6
- sequence_lengths: int32 [2, 8], P('dp'), may hold values from 1 to 512, 1024 in all within a row
Outputs:
- projected: bfloat16 [2048, 8192], P(('dp', 'row'), 'col')
- grad_mag: float32 [8192], P('col')
- input_factor_gradient: float32 [16, 8192], P(None, 'row')
- grad_b: float32 [16, 8192], P(None, 'col')
Inputs may be any that keep to these rules, and one draw needn't show every extreme that they name: `sequence_lengths`: each group's 8 lengths sum to 1024, and one of them is exactly 512.
All inputs are finite; a program needn't handle non-finite values.
Results may differ from a plain program's by a relative error of at most 0.0052.
Values may be sent and summed in bfloat16 or wider, within the bound.
No kernel may reach another device: no remote copies, remote signals or barrier semaphores. Data moves between devices by JAX's collectives and lax.ppermute only.
A program may use at most 64 MiB of HBM per device.

v0:
```python
import jax
import jax.numpy as jnp
from jax import lax
from jax.sharding import PartitionSpec as P

norm_eps = 1e-06
highest_precision = lax.Precision.HIGHEST


def contract_product(left, right, left_dim, right_dim):
    return lax.dot_general(
        left, right, (((left_dim,), (right_dim,)), ((), ())), preferred_element_type=jnp.float32
    )


def per_device(
    tokens,
    frozen_weight,
    input_adapter_factor,
    output_adapter_factor,
    magnitude,
    cotangent,
    sequence_lengths,
):
    row_count = lax.axis_size("row")
    col_count = lax.axis_size("col")
    row_index = lax.axis_index("row")
    col_index = lax.axis_index("col")
    group_index = lax.axis_index("dp")
    local_rows = tokens.shape[0]
    group_rows = local_rows * col_count
    block_rows = group_rows // row_count
    adapter_rank_size = input_adapter_factor.shape[0]
    low_rank_update = contract_product(input_adapter_factor, output_adapter_factor, 0, 0)
    merged = frozen_weight.astype(jnp.float32) + low_rank_update
    norm_terms = jnp.sum(merged * merged, axis=0)
    gram_partial_terms = contract_product(input_adapter_factor, input_adapter_factor, 1, 1)
    merged_factor_terms = jnp.dot(
        input_adapter_factor, frozen_weight, preferred_element_type=jnp.float32
    ) + jnp.dot(
        gram_partial_terms, output_adapter_factor.astype(jnp.float32), precision=highest_precision
    )
    portion = lax.all_gather(tokens, "col", axis=0, tiled=True)
    base_piece = jnp.dot(portion, frozen_weight, preferred_element_type=jnp.float32)
    down_portion = contract_product(portion, input_adapter_factor, 1, 1)
    frozen_rows, down_rows = (
        lax.psum_scatter(base_piece, "row", scatter_dimension=0, tiled=True),
        lax.psum_scatter(down_portion, "row", scatter_dimension=0, tiled=True),
    )
    norm_sq, merged_input_factor = lax.psum((norm_terms, merged_factor_terms), "row")
    down_activations = down_rows.astype(jnp.bfloat16)
    col_norm = jnp.sqrt(norm_sq + norm_eps)
    col_scale = magnitude / col_norm
    query_projection = frozen_rows + jnp.dot(
        down_activations, output_adapter_factor, preferred_element_type=jnp.float32
    )
    projected = (query_projection * col_scale[None, :]).astype(jnp.bfloat16)
    lengths = sequence_lengths[0]
    ends = jnp.cumsum(lengths, dtype=jnp.int32)
    starts = ends - lengths
    positions = row_index * block_rows + jnp.arange(block_rows, dtype=jnp.int32)
    inside = (positions[:, None] >= starts[None, :]) & (positions[:, None] < ends[None, :])
    inverse = 1.0 / lengths.astype(jnp.float32)
    weights = jnp.sum(jnp.where(inside, inverse[None, :], jnp.float32(0.0)), axis=1)
    grad_out = cotangent.astype(jnp.float32) * weights[:, None]
    scale_terms = jnp.sum(grad_out * query_projection, axis=0)
    projection_gradient = (grad_out * col_scale[None, :]).astype(jnp.bfloat16)
    bgrad_terms = contract_product(down_activations, projection_gradient, 0, 0)
    scale_grad, bgrad_data = lax.psum((scale_terms, bgrad_terms), ("dp", "row"))
    grad_mag = scale_grad / col_norm
    norm_coefficient = -scale_grad * magnitude / (col_norm * col_norm * col_norm)
    grad_b = bgrad_data + merged_input_factor * norm_coefficient[None, :]
    backward_terms = contract_product(projection_gradient, output_adapter_factor, 1, 1)
    padded = lax.dynamic_update_slice_in_dim(
        jnp.zeros((group_rows, adapter_rank_size), jnp.float32),
        backward_terms,
        row_index * block_rows,
        0,
    )
    backward_rows = lax.psum(padded, ("row", "col")).astype(jnp.bfloat16)
    back_mine = lax.dynamic_slice_in_dim(backward_rows, col_index * local_rows, local_rows, 0)
    row_term = contract_product(back_mine, tokens, 0, 0)
    scaled_output_factor = (
        output_adapter_factor.astype(jnp.float32) * norm_coefficient[None, :]
    ).astype(jnp.bfloat16)
    norm_term = contract_product(scaled_output_factor, frozen_weight, 1, 1) + jnp.dot(
        contract_product(scaled_output_factor, output_adapter_factor, 1, 1),
        input_adapter_factor.astype(jnp.float32),
        precision=highest_precision,
    )
    first_group = (group_index == 0).astype(jnp.float32)
    input_factor_gradient = lax.psum(row_term + first_group * norm_term, ("dp", "col"))
    return (projected, grad_mag, input_factor_gradient, grad_b)


def solution(mesh):
    in_specs = (
        P(("dp", "col"), "row"),
        P("row", "col"),
        P(None, "row"),
        P(None, "col"),
        P("col"),
        P(("dp", "row"), "col"),
        P("dp", None),
    )
    out_specs = (P(("dp", "row"), "col"), P("col"), P(None, "row"), P(None, "col"))
    return jax.shard_map(
        per_device, mesh=mesh, in_specs=in_specs, out_specs=out_specs, check_vma=False
    )
```

profile of v0, /device:TPU:0, one launch (start us, length us, event | category | flops | bytes accessed | tf_op | source)
XLA Modules:
  0.0 366.2 jit_solution(13270679273868545477)
XLA Ops:
  7.2 0.7 all-gather.2.cloned.1.call-update
  8.0 85.1 %all-gather.2.cloned.1.call-done = bf16[1024,2048]{1,0:T(8,128)(2,1)} async-done(((bf16[256,2048]{1,0:T(8,128)(2,1)}), bf16[1024,2048]{1,0:T(8,128)(2,1)}) %all-gather.2.cloned.1.call-update) | async-done | bytes 4194320 | tf_op jit(solution)/shard_map/all_gather | solution.py:43
  93.1 4.0 %fusion.14 = f32[1024,16]{0,1:T(8,128)} fusion(bf16[1024,2048]{1,0:T(8,128)(2,1)} %all-gather.2.cloned.1.call-done, bf16[16,2048]{1,0:T(8,128)(2,1)S(1)} %copy-done), kind=kOutput, calls=%fused_computation.33 | convolution fusion | flops 67108864 | bytes 4325376 | tf_op jit(solution)/shard_map/dot_general | solution.py:11
  97.1 14.4 %fusion.13 = f32[1024,2048]{1,0:T(8,128)} fusion(bf16[1024,2048]{1,0:T(8,128)(2,1)} %all-gather.2.cloned.1.call-done, bf16[2048,2048]{1,0:T(8,128)(2,1)} %param.8), kind=kOutput, calls=%fused_computation.32 | convolution fusion | flops 8589934592 | bytes 20971520 | tf_op jit(solution)/shard_map/dot_general | solution.py:44
  111.8 4.6 %fusion.15 = f32[16,2048]{1,0:T(8,128)S(1)} fusion(bf16[16,2048]{1,0:T(8,128)(2,1)S(1)} %copy-done, bf16[2048,2048]{1,0:T(8,128)(2,1)} %param.8), kind=kOutput, calls=%fused_computation.34 | convolution fusion | flops 134217728 | bytes 8585216 | tf_op jit(solution)/shard_map/dot_general | solution.py:38
  116.4 0.9 convolution_add_fusion.1
  117.4 5.9 %multiply_reduce_fusion = f32[2048]{0:T(1024)S(1)} fusion(bf16[2048,2048]{1,0:T(8,128)(2,1)} %param.8, bf16[16,2048]{1,0:T(8,128)(2,1)S(1)} %copy-done, bf16[16,2048]{1,0:T(8,128)(2,1)S(1)} %copy-done.2), kind=kOutput, calls=%fused_computation | convolution fusion | flops 150992896 | bytes 8527872 | tf_op jit(solution)/shard_map/dot_general | solution.py:11
  123.3 0.2 reduce-window.4
  123.5 6.5 %psum.42 = f32[2048]{0:T(1024)S(1)} all-reduce(f32[2048]{0:T(1024)S(1)} %multiply_reduce_fusion), channel_id=1, replica_groups=mesh['dp'=2,'row'=4,'col'=4] {'row'}, use_global_device_ids=true, to_apply=%region_3.0 | all-reduce | flops 2048 | bytes 16384 | tf_op jit(solution)/shard_map/psum | solution.py:50
  130.2 0.5 convolution_dynamic-update-slice_fusion
  130.7 69.2 %psum.44 = bf16[1024,16]{1,0:T(8,128)(2,1)S(1)} all-reduce(f32[1024,16]{1,0:T(8,128)S(1)} %convolution_dynamic-update-slice_fusion), channel_id=1, replica_groups=mesh['dp'=2,'row'=4,'col'=4] {'row','col'}, use_global_device_ids=true, to_apply=%region_8.9 | all-reduce | flops 16384 | bytes 98304 | tf_op jit(solution)/shard_map/psum | solution.py:80
  200.0 1.8 fusion.1
  201.9 3.2 multiply_reduce_fusion.1
  205.1 12.1 %psum.43 = f32[2048]{0:T(1024)S(1)} all-reduce(f32[2048]{0:T(1024)S(1)} %get-tuple-element.4), channel_id=1, replica_groups=mesh['dp'=2,'row'=4,'col'=4] {'dp','row'}, use_global_device_ids=true, to_apply=%region_7.8 | all-reduce | flops 2048 | bytes 16384 | tf_op jit(solution)/shard_map/psum | solution.py:69
  217.1 0.6 fusion.6
  217.8 5.7 %fusion.3 = f32[16,2048]{1,0:T(8,128)S(1)} fusion(bf16[2048,2048]{1,0:T(8,128)(2,1)} %param.8, bf16[16,2048]{1,0:T(8,128)(2,1)S(1)} %copy-done.2, f32[2048]{0:T(1024)S(1)} %get-tuple-element.6), kind=kOutput, calls=%fused_computation.16 | convolution fusion | flops 134316032 | bytes 8593408 | tf_op jit(solution)/shard_map/dot_general | solution.py:11
  223.5 0.1 fusion.2
  223.6 0.2 fusion
  223.9 0.9 convolution_add_fusion.3
  224.8 2.4 all-reduce.8.cloned.1.call-done
  227.2 57.0 %all-reduce.6.cloned.1.call-done = f32[16,2048]{1,0:T(8,128)} async-done(((f32[16,2048]{1,0:T(8,128)}), f32[16,2048]{1,0:T(8,128)}) %all-reduce.6.cloned.1.call-update) | async-done | bytes 131088 | tf_op jit(solution)/shard_map/psum | solution.py:69
  284.2 1.6 multiply_add_fusion
  285.9 71.9 %all-reduce.4.cloned.1.call-done = f32[16,2048]{1,0:T(8,128)} async-done(((f32[16,2048]{1,0:T(8,128)}), f32[16,2048]{1,0:T(8,128)}) %all-reduce.4.cloned.1.call-update) | async-done | bytes 131088 | tf_op jit(solution)/shard_map/psum | solution.py:92
  357.8 1.6 copy.15
  (32 shorter events, 0.7 us)
Async XLA Ops:
  7.2 85.9 %copy-start = (bf16[16,2048]{1,0:T(8,128)(2,1)S(1)}, bf16[16,2048]{1,0:T(8,128)(2,1)}, u32[]{:S(2)}) copy-start(bf16[16,2048]{1,0:T(8,128)(2,1)} %param.9) | copy-start | bytes 196612
  7.2 85.9 %all-gather.2.cloned.1.call-start = ((), (), s32[]{:S(2)}) async-start(), calls=%async_computation.2 | async-start | bytes 5242880 | tf_op jit(solution)/shard_map/all_gather | solution.py:43
  7.9 192.0 %reduce-scatter.5.cloned.1.call-start = ((), (), s32[]{:S(2)}) async-start(), calls=%async_computation.4 | async-start | bytes 81920 | tf_op jit(solution)/shard_map/reduce_scatter | solution.py:48
  97.1 104.8 %reduce-scatter.3.cloned.1.call-start = ((), (), s32[]{:S(2)}) async-start(), calls=%async_computation.3 | async-start | bytes 10485760 | tf_op jit(solution)/shard_map/reduce_scatter | solution.py:47
  111.6 115.7 %all-reduce.8.cloned.1.call-start = ((), (), s32[]{:S(2)}) async-start(), calls=%async_computation.7 | async-start | bytes 262144 | tf_op jit(solution)/shard_map/psum | solution.py:50
  111.8 4.6 %copy-start.2 = (bf16[16,2048]{1,0:T(8,128)(2,1)S(1)}, bf16[16,2048]{1,0:T(8,128)(2,1)}, u32[]{:S(2)}) copy-start(bf16[16,2048]{1,0:T(8,128)(2,1)} %param.10) | copy-start | bytes 196612
  117.3 166.9 %all-reduce.6.cloned.1.call-start = ((), (), s32[]{:S(2)}) async-start(), calls=%async_computation.6 | async-start | bytes 262144 | tf_op jit(solution)/shard_map/psum | solution.py:69
  117.3 5.9 %copy-start.5 = (s32[1,8]{1,0:T(1,128)S(1)}, s32[1,8]{1,0:T(1,128)}, u32[]{:S(2)}) copy-start(s32[1,8]{1,0:T(1,128)} %param.13) | copy-start | bytes 100
  117.4 12.7 %copy-start.4 = (f32[2048]{0:T(1024)S(1)}, f32[2048]{0:T(1024)}, u32[]{:S(2)}) copy-start(f32[2048]{0:T(1024)} %param.11) | copy-start | bytes 24580
  117.4 12.8 %copy-start.3 = (bf16[256,2048]{1,0:T(8,128)(2,1)S(1)}, bf16[256,2048]{1,0:T(8,128)(2,1)}, u32[]{:S(2)}) copy-start(bf16[256,2048]{1,0:T(8,128)(2,1)} %param.12) | copy-start | bytes 3145732
  201.8 156.0 %all-reduce.4.cloned.1.call-start = ((), (), s32[]{:S(2)}) async-start(), calls=%async_computation.5 | async-start | bytes 262144 | tf_op jit(solution)/shard_map/psum | solution.py:92
  217.8 6.1 %copy-start.1 = (bf16[256,2048]{1,0:T(8,128)(2,1)S(1)}, bf16[256,2048]{1,0:T(8,128)(2,1)}, u32[]{:S(2)}) copy-start(bf16[256,2048]{1,0:T(8,128)(2,1)} %param.7) | copy-start | bytes 3145732
Sparse Core Ops, SparseCore 0:
  9.6 83.4 all-gather.1
  97.2 18.0 reduce-scatter.4
  117.9 75.6 reduce-scatter.2
  195.8 31.4 all-reduce.7
  230.7 53.4 all-reduce.5
  288.0 69.7 all-reduce.3
where the time goes:
time: 367 us; the launch traced here: 366 us
  waiting for transfers between devices  217 us (59%)
  blocking collectives  87.8 us (24%)
  matrix products  42.5 us (12%)
  between operations  14.3 us (4%)
    all_gather x1, waiting for transfers between devices, per_device(): portion = lax.all_gather(tokens, 'col', axis=0, tiled=True)  85.1 us
    psum x1, waiting for transfers between devices, per_device(): lax.psum(row_term + first_group * norm_term, ('dp', 'col'))  71.9 us
    psum x1, blocking collectives, per_device(): backward_rows = lax.psum(padded, ('row', 'col')).astype(jnp.bfloat16)  69.2 us
    psum x1, waiting for transfers between devices, per_device(): scale_grad, bgrad_data = lax.psum((scale_terms, bgrad_terms), ('dp', 'row'))  57 us
    dot_general x8, matrix products, contract_product(): lax.dot_general(left, right, (((left_dim,), (right_dim,)), ((), ())), pre...  19.1 us
    dot_general x1, matrix products, per_device(): jnp.dot(portion, frozen_weight, preferred_element_type=jnp.float32)  14.4 us
    psum x1, blocking collectives, per_device(): scale_grad, bgrad_data = lax.psum((scale_terms, bgrad_terms), ('dp', 'row'))  12.1 us
  transfers between devices with their start and end apart: 6, of which 4 were waited for; matrix products, arithmetic and copies ran while one was open for 11% of the time, Pallas kernels for 0%

commit v1 on v0

--- a/solution.py
+++ b/solution.py
@@ -5,6 +5,11 @@
 
 norm_eps = 1e-06
 highest_precision = lax.Precision.HIGHEST
+
+
+def by_each_axis(array, axis_one, axis_two):
+    partial = lax.psum(array, axis_one)
+    return lax.psum(partial, axis_two)
 
 
 def contract_product(left, right, left_dim, right_dim):
@@ -66,7 +71,7 @@
     scale_terms = jnp.sum(grad_out * query_projection, axis=0)
     projection_gradient = (grad_out * col_scale[None, :]).astype(jnp.bfloat16)
     bgrad_terms = contract_product(down_activations, projection_gradient, 0, 0)
-    scale_grad, bgrad_data = lax.psum((scale_terms, bgrad_terms), ("dp", "row"))
+    scale_grad, bgrad_data = by_each_axis((scale_terms, bgrad_terms), "dp", "row")
     grad_mag = scale_grad / col_norm
     norm_coefficient = -scale_grad * magnitude / (col_norm * col_norm * col_norm)
     grad_b = bgrad_data + merged_input_factor * norm_coefficient[None, :]

time: 367 us -> 400 us (1.090)
  waiting for transfers between devices: 217 us -> 253 us
    reduce_scatter x1, waiting for transfers between devices: 0.02 us -> 65.2 us  [per_device(): lax.psum_scatter(base_piece, 'row', scatter_dimension=0, tiled=True)]
    psum x2, waiting for transfers between devices: 59.4 us -> 28.9 us  [the longest x1 28.9 us: by_each_axis(): return lax.psum(partial, axis_two)]
    psum x1, blocking collectives: 12.1 us -> 5 us  [by_each_axis(): partial = lax.psum(array, axis_one)]
  transfers between devices with their start and end apart: 6 -> 6, of which waited for: 4 -> 4; matrix products, arithmetic and copies ran while one was open for 11% -> 8% of each run, Pallas kernels for 0% -> 0%
where the time goes in v1:
time: 400 us
  waiting for transfers between devices  253 us (63%)
  blocking collectives  85.2 us (21%)
  matrix products  41.8 us (10%)
  between operations  14.2 us (4%)
    all_gather x1, waiting for transfers between devices, per_device(): portion = lax.all_gather(tokens, 'col', axis=0, tiled=True)  85.1 us
    psum x1, waiting for transfers between devices, per_device(): lax.psum(row_term + first_group * norm_term, ('dp', 'col'))  72.6 us
    psum x1, blocking collectives, per_device(): backward_rows = lax.psum(padded, ('row', 'col')).astype(jnp.bfloat16)  70.1 us
    reduce_scatter x1, waiting for transfers between devices, per_device(): lax.psum_scatter(base_piece, 'row', scatter_dimension=0, tiled=True)  65.2 us
    psum x1, waiting for transfers between devices, by_each_axis(): return lax.psum(partial, axis_two)  28.9 us
    dot_general x8, matrix products, contract_product(): lax.dot_general(left, right, (((left_dim,), (right_dim,)), ((), ())), pre...  19.6 us
    dot_general x1, matrix products, per_device(): jnp.dot(portion, frozen_weight, preferred_element_type=jnp.float32)  14.4 us
    psum x1, blocking collectives, per_device(): lax.psum((norm_terms, merged_factor_terms), 'row')  10.1 us
  transfers between devices with their start and end apart: 6, of which 4 were waited for; matrix products, arithmetic and copies ran while one was open for 8% of the time, Pallas kernels for 0%

profile of v1, /device:TPU:0, one launch (start us, length us, event | category | flops | bytes accessed | tf_op | source)
XLA Modules:
  0.0 399.9 jit_solution(8748427013280661994)
XLA Ops:
  7.2 0.7 all-gather.2.cloned.1.call-update
  8.0 85.1 %all-gather.2.cloned.1.call-done = bf16[1024,2048]{1,0:T(8,128)(2,1)} async-done(((bf16[256,2048]{1,0:T(8,128)(2,1)}), bf16[1024,2048]{1,0:T(8,128)(2,1)}) %all-gather.2.cloned.1.call-update) | async-done | bytes 4194320 | tf_op jit(solution)/shard_map/all_gather | solution.py:48
  93.1 4.0 %fusion.14 = f32[1024,16]{0,1:T(8,128)} fusion(bf16[1024,2048]{1,0:T(8,128)(2,1)} %all-gather.2.cloned.1.call-done, bf16[16,2048]{1,0:T(8,128)(2,1)S(1)} %copy-done), kind=kOutput, calls=%fused_computation.33 | convolution fusion | flops 67108864 | bytes 4325376 | tf_op jit(solution)/shard_map/dot_general | solution.py:16
  97.1 14.4 %fusion.13 = f32[1024,2048]{1,0:T(8,128)} fusion(bf16[1024,2048]{1,0:T(8,128)(2,1)} %all-gather.2.cloned.1.call-done, bf16[2048,2048]{1,0:T(8,128)(2,1)} %param.8), kind=kOutput, calls=%fused_computation.32 | convolution fusion | flops 8589934592 | bytes 20971520 | tf_op jit(solution)/shard_map/dot_general | solution.py:49
  111.7 0.6 copy-done.6
  112.6 4.7 %fusion.15 = f32[16,2048]{1,0:T(8,128)S(1)} fusion(bf16[16,2048]{1,0:T(8,128)(2,1)S(1)} %copy-done, bf16[2048,2048]{1,0:T(8,128)(2,1)} %param.8), kind=kOutput, calls=%fused_computation.34 | convolution fusion | flops 134217728 | bytes 8585216 | tf_op jit(solution)/shard_map/dot_general | solution.py:43
  117.3 0.8 convolution_add_fusion.1
  118.1 5.9 %multiply_reduce_fusion = f32[2048]{0:T(1024)S(1)} fusion(bf16[2048,2048]{1,0:T(8,128)(2,1)} %param.8, bf16[16,2048]{1,0:T(8,128)(2,1)S(1)} %copy-done, bf16[16,2048]{1,0:T(8,128)(2,1)S(1)} %copy-done.2), kind=kOutput, calls=%fused_computation | convolution fusion | flops 150992896 | bytes 8527872 | tf_op jit(solution)/shard_map/dot_general | solution.py:16
  124.1 65.2 %reduce-scatter.3.cloned.1.call-done = f32[256,2048]{1,0:T(8,128)} async-done(((f32[1024,2048]{1,0:T(8,128)}), f32[256,2048]{1,0:T(8,128)}) %reduce-scatter.3.cloned.1.call-update) | async-done | bytes 2097168 | tf_op jit(solution)/shard_map/reduce_scatter | solution.py:52
  189.3 2.1 multiply_reduce_fusion.1
  191.4 5.0 %psum.57 = f32[2048]{0:T(1024)S(1)} all-reduce(f32[2048]{0:T(1024)S(1)} %get-tuple-element.11), channel_id=1, replica_groups=mesh['dp'=2,'row'=4,'col'=4] {'dp'}, use_global_device_ids=true, to_apply=%region_7.8 | all-reduce | flops 2048 | bytes 16384 | tf_op jit(solution)/shard_map/psum | solution.py:11
  196.4 10.1 %all-reduce = (f32[2048]{0:T(1024)S(1)}, f32[2048]{0:T(1024)S(1)}) all-reduce(f32[2048]{0:T(1024)S(1)} %multiply_reduce_fusion, f32[2048]{0:T(1024)S(1)} %psum.57), channel_id=1, replica_groups=mesh['dp'=2,'row'=4,'col'=4] {'row'}, use_global_device_ids=true, to_apply=%region_3.0 | all-reduce | flops 4096 | bytes 32768 | tf_op jit(solution)/shard_map/psum | solution.py:55
  206.6 0.6 fusion.6
  207.2 5.7 %fusion.3 = f32[16,2048]{1,0:T(8,128)S(1)} fusion(bf16[2048,2048]{1,0:T(8,128)(2,1)} %param.8, bf16[16,2048]{1,0:T(8,128)(2,1)S(1)} %copy-done.2, f32[2048]{0:T(1024)S(1)} %get-tuple-element.8), kind=kOutput, calls=%fused_computation.16 | convolution fusion | flops 134316032 | bytes 8593408 | tf_op jit(solution)/shard_map/dot_general | solution.py:16
  213.0 1.1 fusion.1
  214.2 1.2 multiply_convert_fusion.1
  215.4 1.7 convolution_dynamic-update-slice_fusion
  217.1 0.2 fusion
  217.3 70.1 %psum.59 = bf16[1024,16]{1,0:T(8,128)(2,1)S(1)} all-reduce(f32[1024,16]{1,0:T(8,128)S(1)} %convolution_dynamic-update-slice_fusion), channel_id=1, replica_groups=mesh['dp'=2,'row'=4,'col'=4] {'row','col'}, use_global_device_ids=true, to_apply=%region_9.10 | all-reduce | flops 16384 | bytes 98304 | tf_op jit(solution)/shard_map/psum | solution.py:85
  287.5 0.9 convolution_add_fusion.3
  288.4 28.9 %all-reduce.10.cloned.1.call-done = (f32[16,2048]{1,0:T(8,128)}, f32[16,2048]{1,0:T(8,128)}) async-done(((f32[16,2048]{1,0:T(8,128)}, f32[16,2048]{1,0:T(8,128)}), (f32[16,2048]{1,0:T(8,128)}, f32[16,2048]{1,0:T(8,128)})) %all-reduce.10.cloned.1.call-update) | async-done | bytes 262160 | tf_op jit(solution)/shard_map/psum | solution.py:12
  317.3 1.6 multiply_add_fusion
  318.9 72.6 %all-reduce.6.cloned.1.call-done = f32[16,2048]{1,0:T(8,128)} async-done(((f32[16,2048]{1,0:T(8,128)}), f32[16,2048]{1,0:T(8,128)}) %all-reduce.6.cloned.1.call-update) | async-done | bytes 131088 | tf_op jit(solution)/shard_map/psum | solution.py:97
  391.5 1.6 copy.16
  (34 shorter events, 1.0 us)
Async XLA Ops:
  7.2 85.9 %copy-start = (bf16[16,2048]{1,0:T(8,128)(2,1)S(1)}, bf16[16,2048]{1,0:T(8,128)(2,1)}, u32[]{:S(2)}) copy-start(bf16[16,2048]{1,0:T(8,128)(2,1)} %param.9) | copy-start | bytes 196612
  7.2 85.9 %all-gather.2.cloned.1.call-start = ((), (), s32[]{:S(2)}) async-start(), calls=%async_computation.2 | async-start | bytes 5242880 | tf_op jit(solution)/shard_map/all_gather | solution.py:48
  7.9 116.1 %reduce-scatter.5.cloned.1.call-start = ((), (), s32[]{:S(2)}) async-start(), calls=%async_computation.4 | async-start | bytes 81920 | tf_op jit(solution)/shard_map/reduce_scatter | solution.py:53
  97.1 92.2 %reduce-scatter.3.cloned.1.call-start = ((), (), s32[]{:S(2)}) async-start(), calls=%async_computation.3 | async-start | bytes 10485760 | tf_op jit(solution)/shard_map/reduce_scatter | solution.py:52
  111.6 0.7 copy-start.6
  111.6 175.8 %all-reduce.8.cloned.1.call-start = ((), (), s32[]{:S(2)}) async-start(), calls=%async_computation.6 | async-start | bytes 262144 | tf_op jit(solution)/shard_map/psum | solution.py:11
  112.6 4.7 %copy-start.2 = (bf16[16,2048]{1,0:T(8,128)(2,1)S(1)}, bf16[16,2048]{1,0:T(8,128)(2,1)}, u32[]{:S(2)}) copy-start(bf16[16,2048]{1,0:T(8,128)(2,1)} %param.10) | copy-start | bytes 196612
  118.1 71.2 %copy-start.3 = (bf16[256,2048]{1,0:T(8,128)(2,1)S(1)}, bf16[256,2048]{1,0:T(8,128)(2,1)}, u32[]{:S(2)}) copy-start(bf16[256,2048]{1,0:T(8,128)(2,1)} %param.12) | copy-start | bytes 3145732
  124.0 82.6 %copy-start.5 = (f32[2048]{0:T(1024)S(1)}, f32[2048]{0:T(1024)}, u32[]{:S(2)}) copy-start(f32[2048]{0:T(1024)} %param.11) | copy-start | bytes 24580
  207.2 5.8 %copy-start.4 = (f32[256,16]{0,1:T(8,128)S(1)}, f32[256,16]{0,1:T(8,128)}, u32[]{:S(2)}) copy-start(f32[256,16]{0,1:T(8,128)} %reduce-scatter.5.cloned.1.call-done) | copy-start | bytes 49156
  214.1 73.4 %copy-start.1 = (bf16[256,2048]{1,0:T(8,128)(2,1)S(1)}, bf16[256,2048]{1,0:T(8,128)(2,1)}, u32[]{:S(2)}) copy-start(bf16[256,2048]{1,0:T(8,128)(2,1)} %param.7) | copy-start | bytes 3145732
  214.1 103.2 %all-reduce.10.cloned.1.call-start = ((), (), s32[]{:S(2)}) async-start(), calls=%async_computation.7 | async-start | bytes 524288 | tf_op jit(solution)/shard_map/psum | solution.py:12
  287.4 104.1 %all-reduce.6.cloned.1.call-start = ((), (), s32[]{:S(2)}) async-start(), calls=%async_computation.5 | async-start | bytes 262144 | tf_op jit(solution)/shard_map/psum | solution.py:97
Sparse Core Ops, SparseCore 0:
  9.6 83.4 all-gather.1
  97.2 18.0 reduce-scatter.4
  117.9 71.3 reduce-scatter.2
  214.3 21.6 all-reduce.7
  287.5 29.7 all-reduce.9
  321.1 70.4 all-reduce.5
